TPU v7x, 32 devices: a whole 2x2x4 slice. The times are simulated.
32 devices in a mesh: seq: 16 (over z, y, core), exp: 2 (over x).
Axes of the slice: x: 2, y: 2, z: 4, core: 2. Of those that a mesh axis runs over, the one named last changes fastest.
Arguments:
- hidden_in: bfloat16 [6, 6144], P('exp', 'seq'), may hold values from -2 to 2
- queries: bfloat16 [6, 6144], P(None, 'exp'), may hold values from -40 to 40
- key_cache: bfloat16 [6, 8192, 1024], P(None, 'seq', 'exp'), may hold values from -16 to 16
- value_cache: bfloat16 [6, 8192, 1024], P(None, 'seq', 'exp'), may hold values from -6 to 6
- lengths: int32 [6], replicated, may hold values from 2 to 8192
- out_weight: bfloat16 [6144, 6144], P('exp', 'seq'), may hold values from -0.078125 to 0.078125
- norm_gain: float32 [6144], P('seq'), may hold values from 0.1 to 1.9
- router: bfloat16 [6144, 8], P('seq'), may hold values from -0.078125 to 0.078125
- expert_ids: int32 [6, 2], P('exp'), may hold values from 0 to 7, as said below
- capacity: int32 [8], replicated, may hold values from 1 to 3, as said below
- w_gate: bfloat16 [8, 6144, 8192], P('exp', None, 'seq'), may hold values from -0.078125 to 0.078125
- w_up: bfloat16 [8, 6144, 8192], P('exp', None, 'seq'), may hold values from -0.078125 to 0.078125
- w_down: bfloat16 [8, 8192, 6144], P('exp', 'seq'), may hold values from -0.09375 to 0.09375
Outputs:
- layer_out: bfloat16 [6, 6144], P('exp', 'seq')
Inputs may be any that keep to these rules, and one draw needn't show every extreme that they name: lengths[b] counts sequence b's live cache positions, the newest token's included. `expert_ids`: the two experts of a token differ. One expert is named by every token; any other expert is named at most 3 times within one aligned block of 3 tokens. The expert that every token names has capacity 3.
All inputs are finite; a program needn't handle non-finite values.
Results may differ from a plain program's by a relative error of at most 0.0085.
Values may be sent and summed in bfloat16 or wider, within the bound.
A program may use at most 128 MiB of HBM per device.

v0:
```python
import math
import jax
import jax.numpy as jnp
from jax import lax
from jax.sharding import PartitionSpec as P

D = 6144
HEADS = 48
KV_HEADS = 8
HEAD_DIM = 128
EXPERTS = 8
masked_score = -1e30
norm_eps = 1e-05


def joined(value, axis, join):
    pieces = jax.tree.map(lambda part: lax.all_gather(part, axis), value)
    head = jax.tree.map(lambda part: part[0], pieces)
    tail = jax.tree.map(lambda part: part[1:], pieces)
    running, _ = lax.scan(lambda running, share: (join(running, share), None), head, tail)
    return running


def merge_partial_results(left_part, right_part):
    left_maximum_score, left_denom, left_sum = left_part
    right_peak, right_denom, right_sum = right_part
    joint_peak = jnp.maximum(left_maximum_score, right_peak)
    left_factor = jnp.exp(left_maximum_score - joint_peak)
    right_factor = jnp.exp(right_peak - joint_peak)
    return (
        joint_peak,
        left_denom * left_factor + right_denom * right_factor,
        left_sum * left_factor[..., None] + right_sum * right_factor[..., None],
    )


def on_device(
    hidden_in,
    queries,
    key_cache,
    value_cache,
    lengths,
    out_weight,
    norm_gain,
    router,
    expert_ids,
    capacity,
    w_gate,
    w_up,
    w_down,
):
    seq_count = queries.shape[0]
    group_size = HEADS // KV_HEADS
    kv_local = key_cache.shape[2] // HEAD_DIM
    span_local = key_cache.shape[1]
    query_heads = queries.reshape(seq_count, kv_local, group_size, HEAD_DIM)
    key_rows = key_cache.reshape(seq_count, span_local, kv_local, HEAD_DIM)
    value_rows = value_cache.reshape(seq_count, span_local, kv_local, HEAD_DIM).astype(jnp.float32)
    first_place = lax.axis_index("seq") * span_local
    places = first_place + jnp.arange(span_local, dtype=jnp.int32)
    live_mask = (places[None, :] < lengths[:, None])[:, None, None, :]
    scores = jnp.einsum(
        "bkgd,bjkd->bkgj", query_heads, key_rows, preferred_element_type=jnp.float32
    ) * (1.0 / math.sqrt(HEAD_DIM))
    scores = jnp.where(live_mask, scores, masked_score)
    local_peak = jnp.max(scores, axis=-1)
    attn_weights = jnp.where(live_mask, jnp.exp(scores - local_peak[..., None]), 0.0)
    local_sum = jnp.einsum(
        "bkgj,bjkd->bkgd", attn_weights, value_rows, precision=lax.Precision.HIGHEST
    )
    global_peak, denom_sum, weighted = joined(
        (local_peak, jnp.sum(attn_weights, axis=-1), local_sum), "seq", merge_partial_results
    )
    attended = (
        (weighted / denom_sum[..., None])
        .reshape(seq_count, kv_local * group_size * HEAD_DIM)
        .astype(jnp.bfloat16)
    )
    partial_value = jnp.dot(attended, out_weight, preferred_element_type=jnp.float32)
    projected = lax.psum_scatter(partial_value, "exp", scatter_dimension=0, tiled=True)
    residual = hidden_in.astype(jnp.float32) + projected
    gained = residual * norm_gain
    router_wide = router.astype(jnp.float32)
    squares = jnp.sum(residual * residual, axis=-1)
    total_sq = lax.psum(squares, "seq")
    scale_row = lax.rsqrt(total_sq / D + norm_eps)
    logits = lax.psum(
        jnp.dot(gained * scale_row[:, None], router_wide, precision=lax.Precision.HIGHEST), "seq"
    )
    normed = (gained * scale_row[:, None]).astype(jnp.bfloat16)
    row_total = expert_ids.shape[0]
    onehot_int = (
        expert_ids[:, :, None] == jnp.arange(EXPERTS, dtype=jnp.int32)[None, None, :]
    ).astype(jnp.int32)
    name_count = jnp.sum(onehot_int, axis=1)
    row_order = jnp.arange(row_total, dtype=jnp.int32)
    before = (row_order[None, :] < row_order[:, None]).astype(jnp.int32)
    earlier = jnp.dot(before, name_count)
    slot_rank = jnp.sum(onehot_int * earlier[:, None, :], axis=-1)
    slot_limit = jnp.sum(onehot_int * capacity[None, None, :], axis=-1)
    kept_mask = (slot_rank < slot_limit).astype(jnp.float32)
    expert_indicator = onehot_int.astype(jnp.float32)
    chosen = jnp.sum(expert_indicator * logits[:, None, :], axis=-1)
    gate_weight = jax.nn.sigmoid(chosen - chosen[:, ::-1])
    slot_match = (slot_rank[:, :, None] == row_order[None, None, :]).astype(jnp.float32)
    placing = jnp.einsum("rke,rks->esr", expert_indicator * kept_mask[:, :, None], slot_match)
    buffer = jnp.einsum(
        "esr,rd->esd", placing.astype(jnp.bfloat16), normed, preferred_element_type=jnp.float32
    ).astype(jnp.bfloat16)
    dispatched = lax.all_to_all(buffer, "exp", split_axis=0, concat_axis=1, tiled=True)
    shard_rows = lax.all_gather(dispatched, "seq", axis=2, tiled=True)
    gate_next = jnp.einsum("ern,enf->erf", shard_rows, w_gate, preferred_element_type=jnp.float32)
    up_next = jnp.einsum("ern,enf->erf", shard_rows, w_up, preferred_element_type=jnp.float32)
    hidden_act = (jax.nn.silu(gate_next) * up_next).astype(jnp.bfloat16)
    partial_out = jnp.einsum("erf,efd->erd", hidden_act, w_down, preferred_element_type=jnp.float32)
    blend_table = jnp.einsum(
        "rke,rks->esr", expert_indicator * (gate_weight * kept_mask)[:, :, None], slot_match
    )
    reduced_output = lax.psum_scatter(partial_out, "seq", scatter_dimension=2, tiled=True)
    returned = lax.all_to_all(reduced_output, "exp", split_axis=1, concat_axis=0, tiled=True)
    combined = jnp.einsum("esr,esd->rd", blend_table, returned, precision=lax.Precision.HIGHEST)
    return (residual + combined).astype(jnp.bfloat16)


def solution(mesh):
    in_specs = (
        P("exp", "seq"),
        P(None, "exp"),
        P(None, "seq", "exp"),
        P(None, "seq", "exp"),
        P(),
        P("exp", "seq"),
        P("seq"),
        P("seq", None),
        P("exp", None),
        P(),
        P("exp", None, "seq"),
        P("exp", None, "seq"),
        P("exp", "seq", None),
    )
    out_specs = P("exp", "seq")
    return jax.shard_map(
        on_device, mesh=mesh, in_specs=in_specs, out_specs=out_specs, check_vma=False
    )
```

profile of v0, /device:TPU:0, one launch (start us, length us, event | category | flops | bytes accessed | tf_op | source)
XLA Modules:
  0.0 272.3 jit_solution(8240845647066863271)
XLA Ops:
  6.5 1.6 reshape.56
  8.2 0.9 broadcast_compare_fusion
  9.1 1.8 fusion.49
  10.9 1.4 fusion.4
  12.3 0.7 copy.28
  13.1 23.7 %all-gather = f32[96,4,6]{2,1,0:T(4,128)S(1)} all-gather(f32[6,4,6]{2,1,0:T(4,128)S(1)} %get-tuple-element.74), channel_id=2, replica_groups=mesh['seq'=16,'exp'=2] {'seq'}, dimensions={0}, use_global_device_ids=true | all-gather | bytes 9792 | tf_op jit(solution)/shard_map/all_gather | solution.py:17
  36.8 0.2 fusion.20
  37.0 18.4 %all-gather.1 = f32[96,4,6]{2,1,0:T(4,128)S(1)} all-gather(f32[6,4,6]{2,1,0:T(4,128)S(1)} %fusion.20), channel_id=3, replica_groups=mesh['seq'=16,'exp'=2] {'seq'}, dimensions={0}, use_global_device_ids=true | all-gather | bytes 9792 | tf_op jit(solution)/shard_map/all_gather | solution.py:17
  55.5 0.7 dynamic-slice
  57.0 0.9 slice.32
  57.9 2.3 slice.35
  60.3 16.4 %while.14 = (s32[]{:T(128)}, f32[6,4,6]{2,1,0:T(4,128)S(1)}, f32[6,4,6]{2,1,0:T(4,128)S(1)}, f32[6,4,6,128]{3,2,1,0:T(8,128)S(1)}, f32[15,6,4,6]{3,2,1,0:T(4,128...) while((s32[]{:T(128)}, f32[6,4,6]{2,1,0:T(4,128)S(1)}, ...), condition=%wide.region_3.4_spmd, body=%wide.region_2.3_spmd.sunk | while | flops 56162 | bytes 374501 | solution.py:20
  60.3 0.9 constant_dynamic-slice_fusion.2
  61.2 0.1 fusion.70
  61.4 0.9 constant_dynamic-slice_fusion.2
  62.3 0.1 fusion.70
  62.5 0.9 constant_dynamic-slice_fusion.2
  63.4 0.1 fusion.70
  63.6 0.9 constant_dynamic-slice_fusion.2
  64.5 0.1 fusion.70
  64.7 0.9 constant_dynamic-slice_fusion.2
  65.6 0.1 fusion.70
  65.8 0.9 constant_dynamic-slice_fusion.2
  66.7 0.1 fusion.70
  66.9 0.9 constant_dynamic-slice_fusion.2
  67.7 0.1 fusion.70
  67.9 0.9 constant_dynamic-slice_fusion.2
  68.8 0.1 fusion.70
  69.0 0.9 constant_dynamic-slice_fusion.2
  69.9 0.1 fusion.70
  70.1 0.9 constant_dynamic-slice_fusion.2
  71.0 0.1 fusion.70
  71.2 0.9 constant_dynamic-slice_fusion.2
  72.1 0.1 fusion.70
  72.3 0.9 constant_dynamic-slice_fusion.2
  73.2 0.1 fusion.70
  73.4 0.9 constant_dynamic-slice_fusion.2
  74.3 0.1 fusion.70
  74.5 0.9 constant_dynamic-slice_fusion.2
  75.4 0.1 fusion.70
  75.6 0.9 constant_dynamic-slice_fusion.2
  76.5 0.1 fusion.70
  76.8 0.4 fusion.50
  77.2 8.1 %all-reduce = f32[6,384]{1,0:T(8,128)S(1)} all-reduce(f32[6,384]{1,0:T(8,128)S(1)} %fusion.50), channel_id=5, replica_groups=mesh['seq'=16,'exp'=2] {'exp'}, use_global_device_ids=true, to_apply=%region_4.5.clone | all-reduce | flops 2304 | bytes 18432
  85.3 0.1 multiply_reduce_fusion
  85.4 0.1 fusion.40
  85.5 29.5 %psum.14 = f32[3]{0:T(128)S(1)} all-reduce(f32[3]{0:T(128)S(1)} %multiply_reduce_fusion), channel_id=1, replica_groups=mesh['seq'=16,'exp'=2] {'seq'}, use_global_device_ids=true, to_apply=%region_9.10 | all-reduce | flops 3 | bytes 24 | tf_op jit(solution)/shard_map/psum | solution.py:85
  115.0 0.2 fusion.26
  115.2 0.3 select_reduce_fusion
  115.5 29.5 %psum.15 = f32[3,8]{1,0:T(4,128)S(1)} all-reduce(f32[3,8]{1,0:T(4,128)S(1)} %fusion.26), channel_id=1, replica_groups=mesh['seq'=16,'exp'=2] {'seq'}, use_global_device_ids=true, to_apply=%region_10.11 | all-reduce | flops 24 | bytes 192 | tf_op jit(solution)/shard_map/psum | solution.py:87
  145.0 0.2 fusion.30
  145.2 0.3 fusion.19
  145.5 0.2 convolution_convert_fusion
  145.7 6.3 %all_to_all.36 = bf16[8,3,384]{2,1,0:T(4,128)(2,1)S(1)} all-to-all(bf16[8,3,384]{2,1,0:T(4,128)(2,1)S(1)} %copy.33), channel_id=1, replica_groups=mesh['seq'=16,'exp'=2] {'exp'}, dimensions={0} | all-to-all | bytes 36864 | tf_op jit(solution)/shard_map/all_to_all | solution.py:110
  152.0 18.3 %all_gather.27 = bf16[4,6,6144]{2,1,0:T(8,128)(2,1)S(1)} all-gather(bf16[4,6,384]{2,1,0:T(8,128)(2,1)S(1)} %copy.35), channel_id=1, replica_groups=mesh['seq'=16,'exp'=2] {'seq'}, dimensions={2}, use_global_device_ids=true | all-gather | bytes 313344 | tf_op jit(solution)/shard_map/all_gather | solution.py:111
  170.3 9.9 %fusion.51 = f32[4,6,512]{2,1,0:T(8,128)S(1)} fusion(bf16[4,6,6144]{2,1,0:T(8,128)(2,1)S(1)} %all_gather.27, bf16[4,6144,512]{2,1,0:T(8,128)(2,1)} %param.25), kind=kOutput, calls=%fused_computation.70 | convolution fusion | flops 150994944 | bytes 25509888 | tf_op jit(solution)/shard_map/ern,enf->erf/dot_general | solution.py:112
  180.2 9.9 %fusion.16 = bf16[4,6,512]{2,1,0:T(8,128)(2,1)S(1)} fusion(bf16[4,6,6144]{2,1,0:T(8,128)(2,1)S(1)} %all_gather.27, bf16[4,6144,512]{2,1,0:T(8,128)(2,1)} %param.26, f32[4,6,512]{2,1,0:T(8,128)S(1)} %fusion.51), kind=kOutput, calls=%fused_computation.19 | convolution fusion | flops 151068672 | bytes 25534464 | tf_op jit(solution)/shard_map/ern,enf->erf/dot_general | solution.py:113
  190.1 10.9 %fusion.52 = f32[4,6,6144]{2,1,0:T(8,128)} fusion(bf16[4,6,512]{2,1,0:T(8,128)(2,1)S(1)} %fusion.16, bf16[4,512,6144]{2,1,0:T(8,128)(2,1)} %param.27), kind=kOutput, calls=%fused_computation.71 | convolution fusion | flops 150994944 | bytes 25780224 | tf_op jit(solution)/shard_map/erf,efd->erd/dot_general | solution.py:115
  201.1 54.9 %reduce-scatter.2.cloned.1.call-done = f32[4,6,384]{2,1,0:T(8,128)} async-done(((f32[4,6,6144]{2,1,0:T(8,128)}), f32[4,6,384]{2,1,0:T(8,128)}) %reduce-scatter.2.cloned.1.call-update) | async-done | bytes 36880 | tf_op jit(solution)/shard_map/reduce_scatter | solution.py:119
  255.9 1.4 copy.36
  257.4 3.3 %all-to-all-start.1 = ((f32[4,6,384]{2,0,1:T(4,128)}), f32[4,6,384]{2,0,1:T(4,128)S(1)}, u32[]{:S(2)}, u32[]{:S(2)}) async-start(f32[4,6,384]{2,0,1:T(4,128)} %copy.36), calls=%async_computation.2 | async-start | bytes 73728 | tf_op jit(solution)/shard_map/all_to_all | solution.py:120
  260.6 0.3 convolution_bitcast_fusion.1
  260.9 3.7 %all-to-all-done.1 = f32[4,6,384]{2,0,1:T(4,128)S(1)} async-done(((f32[4,6,384]{2,0,1:T(4,128)}), f32[4,6,384]{2,0,1:T(4,128)S(1)}, u32[]{:S(2)}, u32[]{:S(2)}) %all-to-all-start.1) | async-done | bytes 36896 | tf_op jit(solution)/shard_map/all_to_all | solution.py:120
  264.6 0.8 fusion.18
  (59 shorter events, 1.2 us)
Async XLA Ops:
  6.5 2.5 copy-start
  6.5 50.4 %all-gather.5.cloned.1.call-start = ((), (), s32[]{:S(2)}) async-start(), calls=%async_computation.4 | async-start | bytes 1253376 | tf_op jit(solution)/shard_map/all_gather | solution.py:17
  8.2 2.7 %copy-start.2 = (bf16[6,512,512]{2,1,0:T(8,128)(2,1)S(1)}, bf16[6,512,512]{2,1,0:T(8,128)(2,1)}, u32[]{:S(2)}) copy-start(bf16[6,512,512]{2,1,0:T(8,128)(2,1)} %param.18) | copy-start | bytes 9437188
  10.9 44.5 %copy-start.5 = (s32[3,2]{0,1:T(2,128)S(1)}, s32[3,2]{0,1:T(2,128)}, u32[]{:S(2)}) copy-start(s32[3,2]{0,1:T(2,128)} %param.23) | copy-start | bytes 76
  10.9 44.6 %copy-start.9 = (u32[32]{0:T(128)S(1)}, u32[32]{0:T(128)}, u32[]{:S(2)}) copy-start(u32[32]{0:T(128)} %constant.44) | copy-start | bytes 388
  13.0 242.9 %reduce-scatter.2.cloned.1.call-start = ((), (), s32[]{:S(2)}) async-start(), calls=%async_computation.3 | async-start | bytes 835584 | tf_op jit(solution)/shard_map/reduce_scatter | solution.py:119
  37.0 39.8 %copy-start.3 = (bf16[3072,384]{1,0:T(8,128)(2,1)S(1)}, bf16[3072,384]{1,0:T(8,128)(2,1)}, u32[]{:S(2)}) copy-start(bf16[3072,384]{1,0:T(8,128)(2,1)} %param.20) | copy-start | bytes 7077892
  60.2 25.0 %copy-start.4 = (bf16[3,384]{1,0:T(4,128)(2,1)S(1)}, bf16[3,384]{1,0:T(4,128)(2,1)}, u32[]{:S(2)}) copy-start(bf16[3,384]{1,0:T(4,128)(2,1)} %param.15) | copy-start | bytes 6916
  60.3 54.8 %copy-start.7 = (bf16[384,8]{0,1:T(8,128)(2,1)S(1)}, bf16[384,8]{0,1:T(8,128)(2,1)}, u32[]{:S(2)}) copy-start(bf16[384,8]{0,1:T(8,128)(2,1)} %param.22) | copy-start | bytes 18436
  60.3 54.8 %copy-start.8 = (f32[384]{0:T(512)S(1)}, f32[384]{0:T(512)}, u32[]{:S(2)}) copy-start(f32[384]{0:T(512)} %param.21) | copy-start | bytes 4612
  60.3 55.0 %copy-start.6 = (s32[8]{0:T(128)S(1)}, s32[8]{0:T(128)}, u32[]{:S(2)}) copy-start(s32[8]{0:T(128)} %param.24) | copy-start | bytes 100
  190.1 75.3 %copy-start.1 = (bf16[6,512,512]{2,1,0:T(8,128)(2,1)S(1)}, bf16[6,512,512]{2,1,0:T(8,128)(2,1)}, u32[]{:S(2)}) copy-start(bf16[6,512,512]{2,1,0:T(8,128)(2,1)} %param.17) | copy-start | bytes 9437188
  257.4 7.2 %all-to-all-start.1 = ((f32[4,6,384]{2,0,1:T(4,128)}), f32[4,6,384]{2,0,1:T(4,128)S(1)}, u32[]{:S(2)}, u32[]{:S(2)}) async-start(f32[4,6,384]{2,0,1:T(4,128)} %copy.36), calls=%async_computation.2 | async-start | bytes 73728 | tf_op jit(solution)/shard_map/all_to_all | solution.py:120
Sparse Core Ops, SparseCore 0:
  13.1 41.2 all-gather.4
  201.2 54.6 reduce-scatter.1
where the time goes:
time: 273 us; the launch traced here: 272 us
  blocking collectives  134 us (49%)
  waiting for transfers between devices  58.6 us (21%)
  matrix products  36.3 us (13%)
  local copies, waits for them, and re-layouts  21.4 us (8%)
  between operations  14.3 us (5%)
  other arithmetic  4.47 us (2%)
  starting transfers between devices  3.3 us (1%)
    reduce_scatter x1, waiting for transfers between devices, on_device(): lax.psum_scatter(partial_out, 'seq', scatter_dimension=2, tiled=True)  54.9 us
    all_gather x2, blocking collectives, joined(): pieces = jax.tree.map(lambda part: lax.all_gather(part, axis), value)  42.1 us
    psum x1, blocking collectives, on_device(): lax.psum(jnp.dot(gained * scale_row[:, None], router_wide, precision=lax....  29.5 us
    psum x1, blocking collectives, on_device(): total_sq = lax.psum(squares, 'seq')  29.5 us
    all_gather x1, blocking collectives, on_device(): shard_rows = lax.all_gather(dispatched, 'seq', axis=2, tiled=True)  18.3 us
    dynamic_slice x15, local copies, waits for them, and re-layouts, joined(): lax.scan(lambda running, share: (join(running, share), None), head, tail)  13.4 us
    dot_general x1, matrix products, on_device(): jnp.einsum('erf,efd->erd', hidden_act, w_down, preferred_element_type=jnp...  10.9 us
    dot_general x1, matrix products, on_device(): jnp.einsum('ern,enf->erf', shard_rows, w_up, preferred_element_type=jnp.f...  9.94 us
  transfers between devices with their start and end apart: 3, of which 2 were waited for; matrix products, arithmetic and copies ran while one was open for 1% of the time, Pallas kernels for 0%

commit v1 on v0

--- a/solution.py
+++ b/solution.py
@@ -82,7 +82,9 @@
     gained = residual * norm_gain
     router_wide = router.astype(jnp.float32)
     squares = jnp.sum(residual * residual, axis=-1)
-    total_sq = lax.psum(squares, "seq")
+    total_sq = squares
+    for hop in (1, 2, 4, 8):
+        total_sq = total_sq + lax.ppermute(total_sq, "seq", [(dev, dev ^ hop) for dev in range(16)])
     scale_row = lax.rsqrt(total_sq / D + norm_eps)
     logits = lax.psum(
         jnp.dot(gained * scale_row[:, None], router_wide, precision=lax.Precision.HIGHEST), "seq"

time: 273 us -> 257 us (0.941)
  blocking collectives: 134 us -> 104 us
  waiting for transfers between devices: 58.6 us -> 69.5 us
    psum x1 -> x0, blocking collectives: 29.5 us -> none  [on_device(): total_sq = lax.psum(squares, 'seq')]
    ppermute x0 -> x4, waiting for transfers between devices: none -> 11 us  [on_device(): lax.ppermute(total_sq, 'seq', [(dev, dev ^ hop) for dev in range(16)])]
  transfers between devices with their start and end apart: 3 -> 7, of which waited for: 2 -> 6; matrix products, arithmetic and copies ran while one was open for 1% -> 1% of each run, Pallas kernels for 0% -> 0%
where the time goes in v1:
time: 257 us; the launch traced here: 256 us
  blocking collectives  104 us (40%)
  waiting for transfers between devices  69.5 us (27%)
  matrix products  36.3 us (14%)
  local copies, waits for them, and re-layouts  21.4 us (8%)
  between operations  14.3 us (6%)
  starting transfers between devices  5.17 us (2%)
  other arithmetic  4.48 us (2%)
    reduce_scatter x1, waiting for transfers between devices, on_device(): lax.psum_scatter(partial_out, 'seq', scatter_dimension=2, tiled=True)  54.9 us
    all_gather x2, blocking collectives, joined(): pieces = jax.tree.map(lambda part: lax.all_gather(part, axis), value)  42.1 us
    psum x1, blocking collectives, on_device(): lax.psum(jnp.dot(gained * scale_row[:, None], router_wide, precision=lax....  29.5 us
    all_gather x1, blocking collectives, on_device(): shard_rows = lax.all_gather(dispatched, 'seq', axis=2, tiled=True)  18.3 us
    dynamic_slice x15, local copies, waits for them, and re-layouts, joined(): lax.scan(lambda running, share: (join(running, share), None), head, tail)  13.4 us
    ppermute x4, waiting for transfers between devices, on_device(): lax.ppermute(total_sq, 'seq', [(dev, dev ^ hop) for dev in range(16)])  11 us
    dot_general x1, matrix products, on_device(): jnp.einsum('erf,efd->erd', hidden_act, w_down, preferred_element_type=jnp...  10.9 us
    dot_general x1, matrix products, on_device(): jnp.einsum('ern,enf->erf', shard_rows, w_up, preferred_element_type=jnp.f...  9.94 us
  transfers between devices with their start and end apart: 7, of which 6 were waited for; matrix products, arithmetic and copies ran while one was open for 1% of the time, Pallas kernels for 0%

profile of v1, /device:TPU:0, one launch (start us, length us, event | category | flops | bytes accessed | tf_op | source)
XLA Modules:
  0.0 255.7 jit_solution(8989080062421339325)
XLA Ops:
  6.5 1.6 reshape.56
  8.2 0.9 broadcast_compare_fusion
  9.1 1.8 fusion.49
  10.9 1.4 fusion.4
  12.3 0.7 copy.28
  13.1 23.7 %all-gather = f32[96,4,6]{2,1,0:T(4,128)S(1)} all-gather(f32[6,4,6]{2,1,0:T(4,128)S(1)} %get-tuple-element.74), channel_id=2, replica_groups=mesh['seq'=16,'exp'=2] {'seq'}, dimensions={0}, use_global_device_ids=true | all-gather | bytes 9792 | tf_op jit(solution)/shard_map/all_gather | solution.py:17
  36.8 0.2 fusion.20
  37.0 18.4 %all-gather.1 = f32[96,4,6]{2,1,0:T(4,128)S(1)} all-gather(f32[6,4,6]{2,1,0:T(4,128)S(1)} %fusion.20), channel_id=3, replica_groups=mesh['seq'=16,'exp'=2] {'seq'}, dimensions={0}, use_global_device_ids=true | all-gather | bytes 9792 | tf_op jit(solution)/shard_map/all_gather | solution.py:17
  55.5 0.7 dynamic-slice
  57.1 0.9 slice.32
  58.0 2.3 slice.35
  60.4 16.4 %while.14 = (s32[]{:T(128)}, f32[6,4,6]{2,1,0:T(4,128)S(1)}, f32[6,4,6]{2,1,0:T(4,128)S(1)}, f32[6,4,6,128]{3,2,1,0:T(8,128)S(1)}, f32[15,6,4,6]{3,2,1,0:T(4,128...) while((s32[]{:T(128)}, f32[6,4,6]{2,1,0:T(4,128)S(1)}, ...), condition=%wide.region_3.4_spmd, body=%wide.region_2.3_spmd.sunk | while | flops 56162 | bytes 374501 | solution.py:20
  60.4 0.9 constant_dynamic-slice_fusion.2
  61.3 0.1 fusion.70
  61.5 0.9 constant_dynamic-slice_fusion.2
  62.4 0.1 fusion.70
  62.6 0.9 constant_dynamic-slice_fusion.2
  63.5 0.1 fusion.70
  63.7 0.9 constant_dynamic-slice_fusion.2
  64.6 0.1 fusion.70
  64.8 0.9 constant_dynamic-slice_fusion.2
  65.7 0.1 fusion.70
  65.9 0.9 constant_dynamic-slice_fusion.2
  66.8 0.1 fusion.70
  67.0 0.9 constant_dynamic-slice_fusion.2
  67.9 0.1 fusion.70
  68.0 0.9 constant_dynamic-slice_fusion.2
  68.9 0.1 fusion.70
  69.1 0.9 constant_dynamic-slice_fusion.2
  70.0 0.1 fusion.70
  70.2 0.9 constant_dynamic-slice_fusion.2
  71.3 0.9 constant_dynamic-slice_fusion.2
  72.2 0.1 fusion.70
  72.4 0.9 constant_dynamic-slice_fusion.2
  73.3 0.1 fusion.70
  73.5 0.9 constant_dynamic-slice_fusion.2
  74.6 0.9 constant_dynamic-slice_fusion.2
  75.5 0.1 fusion.70
  75.7 0.9 constant_dynamic-slice_fusion.2
  76.6 0.1 fusion.70
  76.9 0.4 fusion.50
  77.3 8.1 %all-reduce = f32[6,384]{1,0:T(8,128)S(1)} all-reduce(f32[6,384]{1,0:T(8,128)S(1)} %fusion.50), channel_id=5, replica_groups=mesh['seq'=16,'exp'=2] {'exp'}, use_global_device_ids=true, to_apply=%region_4.5.clone | all-reduce | flops 2304 | bytes 18432
  85.6 1.1 collective-permute-done
  86.7 1.8 collective-permute-start.1
  88.5 1.8 collective-permute-done.1
  90.3 3.6 %collective-permute-done.2 = f32[3]{0:T(128)S(1)} collective-permute-done((f32[3]{0:T(128)S(1)}, f32[3]{0:T(128)S(1)}, u32[]{:S(2)}, u32[]{:S(2)}) %collective-permute-start.2) | collective-permute-done | bytes 44 | tf_op jit(solution)/shard_map/ppermute | solution.py:87
  93.9 4.5 %collective-permute-done.3 = f32[3]{0:T(128)S(1)} collective-permute-done((f32[3]{0:T(128)S(1)}, f32[3]{0:T(128)S(1)}, u32[]{:S(2)}, u32[]{:S(2)}) %collective-permute-start.3) | collective-permute-done | bytes 44 | tf_op jit(solution)/shard_map/ppermute | solution.py:87
  98.4 0.2 fusion.26
  98.6 0.3 select_reduce_fusion
  98.8 29.5 %psum.7 = f32[3,8]{1,0:T(4,128)S(1)} all-reduce(f32[3,8]{1,0:T(4,128)S(1)} %fusion.26), channel_id=1, replica_groups=mesh['seq'=16,'exp'=2] {'seq'}, use_global_device_ids=true, to_apply=%region_9.10 | all-reduce | flops 24 | bytes 192 | tf_op jit(solution)/shard_map/psum | solution.py:89
  128.3 0.2 fusion.30
  128.6 0.3 fusion.19
  128.9 0.2 convolution_convert_fusion
  129.1 6.3 %all_to_all.36 = bf16[8,3,384]{2,1,0:T(4,128)(2,1)S(1)} all-to-all(bf16[8,3,384]{2,1,0:T(4,128)(2,1)S(1)} %copy.33), channel_id=1, replica_groups=mesh['seq'=16,'exp'=2] {'exp'}, dimensions={0} | all-to-all | bytes 36864 | tf_op jit(solution)/shard_map/all_to_all | solution.py:112
  135.4 18.3 %all_gather.27 = bf16[4,6,6144]{2,1,0:T(8,128)(2,1)S(1)} all-gather(bf16[4,6,384]{2,1,0:T(8,128)(2,1)S(1)} %copy.35), channel_id=1, replica_groups=mesh['seq'=16,'exp'=2] {'seq'}, dimensions={2}, use_global_device_ids=true | all-gather | bytes 313344 | tf_op jit(solution)/shard_map/all_gather | solution.py:113
  153.7 9.9 %fusion.51 = f32[4,6,512]{2,1,0:T(8,128)S(1)} fusion(bf16[4,6,6144]{2,1,0:T(8,128)(2,1)S(1)} %all_gather.27, bf16[4,6144,512]{2,1,0:T(8,128)(2,1)} %param.25), kind=kOutput, calls=%fused_computation.70 | convolution fusion | flops 150994944 | bytes 25509888 | tf_op jit(solution)/shard_map/ern,enf->erf/dot_general | solution.py:114
  163.6 9.9 %fusion.16 = bf16[4,6,512]{2,1,0:T(8,128)(2,1)S(1)} fusion(bf16[4,6,6144]{2,1,0:T(8,128)(2,1)S(1)} %all_gather.27, bf16[4,6144,512]{2,1,0:T(8,128)(2,1)} %param.26, f32[4,6,512]{2,1,0:T(8,128)S(1)} %fusion.51), kind=kOutput, calls=%fused_computation.19 | convolution fusion | flops 151068672 | bytes 25534464 | tf_op jit(solution)/shard_map/ern,enf->erf/dot_general | solution.py:115
  173.5 10.9 %fusion.52 = f32[4,6,6144]{2,1,0:T(8,128)} fusion(bf16[4,6,512]{2,1,0:T(8,128)(2,1)S(1)} %fusion.16, bf16[4,512,6144]{2,1,0:T(8,128)(2,1)} %param.27), kind=kOutput, calls=%fused_computation.71 | convolution fusion | flops 150994944 | bytes 25780224 | tf_op jit(solution)/shard_map/erf,efd->erd/dot_general | solution.py:117
  184.5 54.9 %reduce-scatter.2.cloned.1.call-done = f32[4,6,384]{2,1,0:T(8,128)} async-done(((f32[4,6,6144]{2,1,0:T(8,128)}), f32[4,6,384]{2,1,0:T(8,128)}) %reduce-scatter.2.cloned.1.call-update) | async-done | bytes 36880 | tf_op jit(solution)/shard_map/reduce_scatter | solution.py:121
  239.3 1.4 copy.36
  240.8 3.3 %all-to-all-start.1 = ((f32[4,6,384]{2,0,1:T(4,128)}), f32[4,6,384]{2,0,1:T(4,128)S(1)}, u32[]{:S(2)}, u32[]{:S(2)}) async-start(f32[4,6,384]{2,0,1:T(4,128)} %copy.36), calls=%async_computation.2 | async-start | bytes 73728 | tf_op jit(solution)/shard_map/all_to_all | solution.py:122
  244.0 0.3 convolution_bitcast_fusion.1
  244.3 3.7 %all-to-all-done.1 = f32[4,6,384]{2,0,1:T(4,128)S(1)} async-done(((f32[4,6,384]{2,0,1:T(4,128)}), f32[4,6,384]{2,0,1:T(4,128)S(1)}, u32[]{:S(2)}, u32[]{:S(2)}) %all-to-all-start.1) | async-done | bytes 36896 | tf_op jit(solution)/shard_map/all_to_all | solution.py:122
  248.0 0.8 fusion.18
  (69 shorter events, 1.8 us)
Async XLA Ops:
  6.5 2.5 copy-start
  6.5 50.6 %all-gather.5.cloned.1.call-start = ((), (), s32[]{:S(2)}) async-start(), calls=%async_computation.4 | async-start | bytes 1253376 | tf_op jit(solution)/shard_map/all_gather | solution.py:17
  8.2 2.7 %copy-start.2 = (bf16[6,512,512]{2,1,0:T(8,128)(2,1)S(1)}, bf16[6,512,512]{2,1,0:T(8,128)(2,1)}, u32[]{:S(2)}) copy-start(bf16[6,512,512]{2,1,0:T(8,128)(2,1)} %param.18) | copy-start | bytes 9437188
  10.9 44.5 %copy-start.5 = (s32[3,2]{0,1:T(2,128)S(1)}, s32[3,2]{0,1:T(2,128)}, u32[]{:S(2)}) copy-start(s32[3,2]{0,1:T(2,128)} %param.23) | copy-start | bytes 76
  10.9 44.6 %copy-start.9 = (u32[32]{0:T(128)S(1)}, u32[32]{0:T(128)}, u32[]{:S(2)}) copy-start(u32[32]{0:T(128)} %constant.44) | copy-start | bytes 388
  13.0 226.3 %reduce-scatter.2.cloned.1.call-start = ((), (), s32[]{:S(2)}) async-start(), calls=%async_computation.3 | async-start | bytes 835584 | tf_op jit(solution)/shard_map/reduce_scatter | solution.py:121
  37.0 39.9 %copy-start.3 = (bf16[3072,384]{1,0:T(8,128)(2,1)S(1)}, bf16[3072,384]{1,0:T(8,128)(2,1)}, u32[]{:S(2)}) copy-start(bf16[3072,384]{1,0:T(8,128)(2,1)} %param.20) | copy-start | bytes 7077892
  60.4 25.0 %copy-start.4 = (bf16[3,384]{1,0:T(4,128)(2,1)S(1)}, bf16[3,384]{1,0:T(4,128)(2,1)}, u32[]{:S(2)}) copy-start(bf16[3,384]{1,0:T(4,128)(2,1)} %param.15) | copy-start | bytes 6916
  60.4 38.0 %copy-start.7 = (bf16[384,8]{0,1:T(8,128)(2,1)S(1)}, bf16[384,8]{0,1:T(8,128)(2,1)}, u32[]{:S(2)}) copy-start(bf16[384,8]{0,1:T(8,128)(2,1)} %param.22) | copy-start | bytes 18436
  60.4 38.0 %copy-start.8 = (f32[384]{0:T(512)S(1)}, f32[384]{0:T(512)}, u32[]{:S(2)}) copy-start(f32[384]{0:T(512)} %param.21) | copy-start | bytes 4612
  60.4 38.2 %copy-start.6 = (s32[8]{0:T(128)S(1)}, s32[8]{0:T(128)}, u32[]{:S(2)}) copy-start(s32[8]{0:T(128)} %param.24) | copy-start | bytes 100
  85.5 1.2 collective-permute-start
  86.7 3.6 %collective-permute-start.1 = (f32[3]{0:T(128)S(1)}, f32[3]{0:T(128)S(1)}, u32[]{:S(2)}, u32[]{:S(2)}) collective-permute-start(f32[3]{0:T(128)S(1)} %add.56), channel_id=1, source_target_pairs={{0,4},{2,6},{4,0},{6,2},{8,12},{10,14},{12,8},{14,10},{16,20},{18,... | collective-permute-start | bytes 44 | tf_op jit(solution)/shard_map/ppermute | solution.py:87
  90.3 3.6 %collective-permute-start.2 = (f32[3]{0:T(128)S(1)}, f32[3]{0:T(128)S(1)}, u32[]{:S(2)}, u32[]{:S(2)}) collective-permute-start(f32[3]{0:T(128)S(1)} %add.57), channel_id=1, source_target_pairs={{0,8},{2,10},{4,12},{6,14},{8,0},{10,2},{12,4},{14,6},{16,24},{18,... | collective-permute-start | bytes 44 | tf_op jit(solution)/shard_map/ppermute | solution.py:87
  93.9 4.5 %collective-permute-start.3 = (f32[3]{0:T(128)S(1)}, f32[3]{0:T(128)S(1)}, u32[]{:S(2)}, u32[]{:S(2)}) collective-permute-start(f32[3]{0:T(128)S(1)} %add.58), channel_id=1, source_target_pairs={{0,16},{2,18},{4,20},{6,22},{8,24},{10,26},{12,28},{14,30},{16,0},... | collective-permute-start | bytes 44 | tf_op jit(solution)/shard_map/ppermute | solution.py:87
  173.5 75.3 %copy-start.1 = (bf16[6,512,512]{2,1,0:T(8,128)(2,1)S(1)}, bf16[6,512,512]{2,1,0:T(8,128)(2,1)}, u32[]{:S(2)}) copy-start(bf16[6,512,512]{2,1,0:T(8,128)(2,1)} %param.17) | copy-start | bytes 9437188
  240.8 7.2 %all-to-all-start.1 = ((f32[4,6,384]{2,0,1:T(4,128)}), f32[4,6,384]{2,0,1:T(4,128)S(1)}, u32[]{:S(2)}, u32[]{:S(2)}) async-start(f32[4,6,384]{2,0,1:T(4,128)} %copy.36), calls=%async_computation.2 | async-start | bytes 73728 | tf_op jit(solution)/shard_map/all_to_all | solution.py:122
Sparse Core Ops, SparseCore 0:
  13.1 41.2 all-gather.4
  184.6 54.6 reduce-scatter.1
